TPU v7x, 16 devices: a 4x2x1 block of a 4x4x8 slice. The times are simulated.
16 devices in a mesh: rep: 2 (over y, z), vocab: 8 (over x, core).
Axes of the slice: x: 4, y: 2, z: 1, core: 2. Of those that a mesh axis runs over, the one named last changes fastest.
The devices are a block of a 4x4x8 slice.
Arguments:
- hidden: bfloat16 [8192, 2304], P(('rep', 'vocab')), parts along dimension 0
- w_head: bfloat16 [256000, 2304], P('vocab')
- allowed_ids: int32 [4096], P('rep'), parts along dimension 0
- allowed_valid: int32 [4096], P('rep'), parts along dimension 0
- target_pos: int32 [8192], P(('rep', 'vocab')), parts along dimension 0
Outputs:
- output 1: float32 [8192, 2048], P(('rep', 'vocab')), parts along dimension 0
- output 2: float32 [8192], P(('rep', 'vocab')), parts along dimension 0
There are 2 independent parts. A program takes and returns all parts, laid end to end along the dimension named above; an argument that names none is the same for every part.
All inputs are finite; a program needn't handle non-finite values.
Results may differ from a plain program's by a relative error of at most 0.001.
Values are sent between devices in bfloat16 or wider.
A program may use at most 768 MiB of HBM per device.

v0:
```python
import functools

import jax
import jax.numpy as jnp
from jax import lax
from jax.experimental import pallas as pl
from jax.experimental.pallas import tpu as pltpu
from jax.sharding import PartitionSpec as P

INV_TEMP = 1.25
MESH = pl.DeviceIdType.MESH
CHUNK = 64
LAG = 2
GATHER = 32
PACK_BITS = 1
PACK = 1 << PACK_BITS
SCORED = 128
PIECES = 2
STAGES = 4
CUT = 768


def gather_kernel(shards, base_ref, sid_ref, w_ref, gbuf_ref, stage, pick, in_sem):
    v = lax.axis_index('vocab')
    vocab_local = w_ref.shape[0]
    half = gbuf_ref.shape[1]
    chip = v // 2

    def span(k):
        at = k * (shards + 1)
        first = base_ref[at + v]
        count = base_ref[at + v + 1] - first
        slot0 = first - base_ref[at + 2 * chip]
        block0 = slot0 // GATHER
        blocks = jnp.where(count > 0, (slot0 + count + GATHER - 1) // GATHER - block0, 0)
        return first, count, slot0, block0, blocks

    spans = [span(0), span(1)]
    total = spans[0][4] + spans[1][4]

    def where_is(t):
        second = t >= spans[0][4]
        first, count, slot0, block0 = [jnp.where(second, spans[1][i], spans[0][i]) for i in range(4)]
        k = jnp.where(second, 1, 0)
        block = block0 + jnp.where(second, t - spans[0][4], t)
        lo = jnp.maximum(slot0 - block * GATHER, 0)
        last = jnp.minimum(slot0 + count - block * GATHER, GATHER) - 1
        src = first + block * GATHER - slot0
        return k, block, lo, last, src

    def row_copy(group, s, b):
        return pltpu.make_async_copy(
            w_ref.at[pl.ds(pl.multiple_of(group * PACK, PACK), PACK), :],
            stage.at[b, s],
            in_sem.at[b])

    lane = lax.broadcasted_iota(jnp.int32, (1, GATHER * PACK), 1)

    def issue(t, b):
        k, first, last, src = where_is(t)[0], *where_is(t)[2:]
        for s in range(GATHER):
            local = sid_ref[k, src + jnp.clip(s, first, last)] - v * vocab_local
            group = lax.shift_right_logical(local, PACK_BITS)
            row_copy(group, s, b).start()
            pick[b, pl.ds(s, 1), :] = jnp.where(lane == s * PACK + (local & (PACK - 1)), 1.0, 0.0)

    def begin(t, carry):
        issue(t, t)
        return carry

    def wait_stage(b):
        pltpu.make_async_copy(stage.at[b], stage.at[b], in_sem.at[b]).wait()

    def step(t, carry):
        b = lax.rem(t, STAGES)

        @pl.when(t + STAGES - 1 < total)
        def _():
            issue(t + STAGES - 1, lax.rem(t + STAGES - 1, STAGES))

        wait_stage(b)
        k, block = where_is(t)[:2]
        gbuf_ref[k, pl.ds(pl.multiple_of(block * GATHER, GATHER), GATHER), :] = jnp.dot(
            pick[b].astype(jnp.bfloat16), stage[b].reshape(GATHER * PACK, stage.shape[3]),
            preferred_element_type=jnp.float32).astype(gbuf_ref.dtype)
        return carry

    lax.fori_loop(0, jnp.minimum(total, STAGES - 1), begin, 0)
    lax.fori_loop(0, total, step, 0)


def ring_kernel(shards, base_ref, rank_ref, hid, gbuf_ref, out_ref,
                other, land, merged, theirs, slot_of, shift, older, newer,
                other_send, other_recv, ring_send, ring_recv, pair_send, pair_recv):
    chips = shards // 2
    half = gbuf_ref.shape[1]
    lag_rows = LAG * CHUNK
    n_own = half // CHUNK
    n_wire = n_own + (chips - 2) * LAG
    n_all = n_own + (chips - 1) * LAG
    max_delay = half // CHUNK + 1
    group = SCORED // CHUNK
    pad = -n_all % group
    gap = group // PIECES
    depth = hid.shape[1]
    v = lax.axis_index('vocab')
    core = lax.rem(v, 2)
    chip = v // 2
    partner = chip * 2 + 1 - core
    ahead = lax.rem(chip + 2 * core - 1 + chips, chips) * 2 + core
    behind = lax.rem(chip - 2 * core + 1 + chips, chips) * 2 + core

    barrier = pltpu.get_barrier_semaphore()
    for peer in (partner, ahead, behind):
        pl.semaphore_signal(barrier, inc=1, device_id={'vocab': peer}, device_id_type=MESH)

    def rows(e, n=CHUNK):
        return pl.ds(pl.multiple_of(e * CHUNK, CHUNK), n)

    def other_copy(e):
        return pltpu.make_async_remote_copy(
            src_ref=gbuf_ref.at[1 - core, rows(e), :], dst_ref=other.at[rows(e), :],
            send_sem=other_send.at[e], recv_sem=other_recv.at[e], device_id={'vocab': partner}, device_id_type=MESH)

    def ring_copy(e):
        return pltpu.make_async_remote_copy(
            src_ref=merged.at[rows(e + pad), :], dst_ref=land.at[rows(e), :],
            send_sem=ring_send.at[e], recv_sem=ring_recv.at[e], device_id={'vocab': ahead}, device_id_type=MESH)

    def pair_copy(e):
        return pltpu.make_async_remote_copy(
            src_ref=merged.at[rows(e + pad), :], dst_ref=theirs.at[rows(e + pad), :],
            send_sem=pair_send.at[e], recv_sem=pair_recv.at[e], device_id={'vocab': partner}, device_id_type=MESH)

    def base(k, w):
        return base_ref[k * (shards + 1) + w]

    pl.semaphore_wait(barrier, 3)
    ahead_of_use = 3
    for e in range(ahead_of_use):
        other_copy(e).start()

    for k in range(2):
        rank = rank_ref[pl.ds(k, 1), :]
        slots = jnp.zeros_like(rank)
        passed = jnp.int32(0)
        for hop in range(chips):
            owner = lax.rem(chip - (2 * k - 1) * hop + chips, chips)
            low, high = base(k, 2 * owner), base(k, 2 * owner + 2)
            slots += jnp.where((rank >= low) & (rank < high), rank + (passed - low), 0)
            passed += jnp.maximum(high - low, lag_rows)
        slot_of[k] = slots + pad * CHUNK
    if pad:
        merged[pl.ds(0, pad * CHUNK), :] = jnp.zeros((pad * CHUNK, depth), merged.dtype)
        theirs[pl.ds(0, pad * CHUNK), :] = jnp.zeros((pad * CHUNK, depth), theirs.dtype)
    older[...] = jnp.zeros_like(older)
    newer[...] = jnp.zeros_like(newer)

    chip_low = base(core, 2 * chip)
    own_pad = jnp.maximum(base(core, 2 * chip + 2) - chip_low, lag_rows)
    delay = (own_pad + CHUNK - 1) // CHUNK
    row = lax.broadcasted_iota(jnp.int32, (CHUNK, 2 * CHUNK), 0)
    col = lax.broadcasted_iota(jnp.int32, (CHUNK, 2 * CHUNK), 1)
    shift[...] = jnp.where(col == row + delay * CHUNK - own_pad, 1.0, 0.0).astype(jnp.bfloat16)
    mine_low = base(core, v) - chip_low
    mine_high = base(core, v + 1) - chip_low
    other_low = base(core, partner) - chip_low
    other_high = base(core, partner + 1) - chip_low

    def move(k, s, p, at, n):
        top = s.astype(jnp.bfloat16)
        rest = s - top.astype(jnp.float32)
        mid = rest.astype(jnp.bfloat16)
        low = (rest - mid.astype(jnp.float32)).astype(jnp.bfloat16)
        slot = lax.broadcasted_iota(jnp.int32, (SCORED, half), 0) + p * SCORED
        place = jnp.where(slot == slot_of[k], 1.0, 0.0).astype(jnp.bfloat16)
        moved = jnp.dot(jnp.concatenate([top, mid, low], axis=1), jnp.concatenate([place] * 3, axis=0),
                        preferred_element_type=jnp.float32)
        spot = (pl.ds(at, n), pl.ds(pl.multiple_of(k * half, half), half))
        out_ref[spot] = out_ref[spot] + moved

    def group_rows(p):
        return pl.ds(pl.multiple_of(p * SCORED, SCORED), SCORED)

    def against(at, n, part):
        return lax.dot_general(hid[pl.ds(at, n), :], part, (((1,), (1,)), ((), ())), preferred_element_type=jnp.float32) * INV_TEMP

    n_rows = hid.shape[0]

    def score(p, at, n):
        s = against(at, n, jnp.concatenate([merged[group_rows(p), :], theirs[group_rows(p), :]], axis=0))
        move(core, s[:, :SCORED], p, at, n)
        move(1 - core, s[:, SCORED:], p, at, n)

    def wait_theirs(p):
        for j in range(group):
            at = p * group + j - pad

            @pl.when(at >= 0)
            def _():
                pair_copy(at).wait_recv()

    def step(e, carry):
        @pl.when(e + ahead_of_use < n_own)
        def _():
            other_copy(e + ahead_of_use).start()

        @pl.when(e < n_own)
        def _():
            other_copy(e).wait_recv()

        @pl.when(e >= LAG)
        def _():
            ring_copy(e - LAG).wait_recv()
            for cut in range(depth // CUT):
                cols = pl.ds(cut * CUT, CUT)
                fresh = land[rows(e - LAG), cols]
                older[:, cols] = jnp.where(delay == LAG, fresh, older[:, cols])
                newer[:, cols] = jnp.where(delay == LAG + 1, fresh, newer[:, cols])

        slot = lax.broadcasted_iota(jnp.int32, (CHUNK, 1), 0) + e * CHUNK
        is_mine = (slot >= mine_low) & (slot < mine_high)
        is_other = (slot >= other_low) & (slot < other_high)
        e_own = jnp.minimum(e, n_own - 1)
        zero = jnp.zeros((), jnp.float32)
        for cut in range(depth // CUT):
            cols = pl.ds(cut * CUT, CUT)
            first, second = older[:, cols], newer[:, cols]
            older[:, cols] = second
            forward = jnp.dot(shift[...], jnp.concatenate([first, second], axis=0), preferred_element_type=jnp.float32)
            from_mine = jnp.where(is_mine, gbuf_ref[core, rows(e_own), cols].astype(jnp.float32), zero)
            from_other = jnp.where(is_other, other[rows(e_own), cols].astype(jnp.float32), zero)
            merged[rows(e + pad), cols] = (from_mine + from_other + forward).astype(jnp.bfloat16)

        @pl.when(e < n_wire)
        def _():
            ring_copy(e).start()

        pair_copy(e).start()

        for cut in range(depth // CUT):
            cols = pl.ds(cut * CUT, CUT)

            def pick(c, acc):
                return jnp.where(c == e + 2 - delay, land[rows(c), cols], acc)

            newer[:, cols] = lax.fori_loop(jnp.maximum(e + 2 - max_delay, 0), e - LAG + 1, pick,
                                           jnp.zeros((CHUNK, CUT), land.dtype))

        @pl.when(e == 0)
        def _():
            out_ref[...] = jnp.zeros_like(out_ref)

        since = e - (group - 1 - pad)

        @pl.when((since >= gap) & (lax.rem(since, gap) == 0) & (e < n_all - 1))
        def _():
            p = (since // gap - 1) // PIECES
            piece = lax.rem(since // gap - 1, PIECES)

            @pl.when(piece == 0)
            def _():
                wait_theirs(p)

            def one(i, c):
                score(p, pl.multiple_of(i * (n_rows // PIECES), n_rows // PIECES), n_rows // PIECES)
                return c

            lax.fori_loop(piece, jnp.where(e == n_all - 2, PIECES, piece + 1), one, 0)

        return carry

    lax.fori_loop(0, n_all, step, 0)

    last = (n_all + pad) // group - 1
    move(core, against(0, n_rows, merged[group_rows(last), :]), last, 0, n_rows)
    wait_theirs(last)
    move(1 - core, against(0, n_rows, theirs[group_rows(last), :]), last, 0, n_rows)

    def finish(e, c):
        @pl.when(e < n_own)
        def _():
            other_copy(e).wait_send()

        @pl.when(e < n_wire)
        def _():
            ring_copy(e).wait_send()

        pair_copy(e).wait_send()
        return c

    lax.fori_loop(0, n_all, finish, 0)


def softmax_kernel(s_ref, valid_ref, target_ref, probs_ref, logp_ref):
    n = probs_ref.shape[0]
    s = s_ref[pl.ds(pl.multiple_of(pl.program_id(0) * n, n), n), :]
    eye = lax.broadcasted_iota(jnp.int32, (n, n), 0) == lax.broadcasted_iota(jnp.int32, (n, n), 1)
    target = jnp.sum(jnp.where(eye, target_ref[0], 0), axis=1, keepdims=True)
    masked = jnp.where(valid_ref[...] > 0, s, -jnp.inf)
    top = jnp.max(masked, axis=1, keepdims=True)
    power = jnp.exp(masked - top)
    total = jnp.sum(power, axis=1, keepdims=True)
    probs_ref[...] = power * (1.0 / total)
    lane = lax.broadcasted_iota(jnp.int32, s.shape, 1)
    picked = jnp.sum(jnp.where(lane == target, s, 0.0), axis=1, keepdims=True)
    logp = picked - (jnp.log(total) + top)
    logp_ref[0] = jnp.sum(jnp.where(eye, logp, 0.0), axis=0, keepdims=True)


def solution(mesh):
    shards = mesh.shape['vocab']

    def device_step(hidden, w_head, allowed_ids, allowed_valid, target_pos):
        list_len = allowed_ids.shape[0]
        half = list_len // 2
        vocab_local, depth = w_head.shape
        rows_dev = hidden.shape[0]
        chips = shards // 2
        ids = allowed_ids.reshape(2, half)
        rank = jnp.sum((ids[:, :, None] < ids[:, None, :]).astype(jnp.int32), axis=1)
        at = lax.broadcasted_iota(jnp.int32, (2, half, half), 1)
        sorted_ids = jnp.sum(jnp.where(rank[:, None, :] == at, ids[:, None, :], 0), axis=2)
        edges = lax.broadcasted_iota(jnp.int32, (2, shards + 1, half), 1) * vocab_local
        base = jnp.sum((ids[:, None, :] < edges).astype(jnp.int32).reshape(2 * (shards + 1), half), axis=1)

        gbuf = pl.pallas_call(
            functools.partial(gather_kernel, shards),
            out_shape=jax.ShapeDtypeStruct((2, half, depth), w_head.dtype),
            in_specs=[pl.BlockSpec(memory_space=pltpu.SMEM), pl.BlockSpec(memory_space=pltpu.SMEM), pl.BlockSpec(memory_space=pl.ANY)],
            out_specs=pl.BlockSpec(memory_space=pltpu.VMEM),
            scratch_shapes=[
                pltpu.VMEM((STAGES, GATHER, PACK, depth), w_head.dtype),
                pltpu.VMEM((STAGES, GATHER, GATHER * PACK), jnp.float32),
                pltpu.SemaphoreType.DMA((STAGES,)),
            ],
            compiler_params=pltpu.CompilerParams(vmem_limit_bytes=20 * 1024 * 1024),
            name='gather_rows',
        )(base, sorted_ids, w_head)

        n_own = half // CHUNK
        n_wire = n_own + (chips - 2) * LAG
        n_all = n_own + (chips - 1) * LAG
        scores = pl.pallas_call(
            functools.partial(ring_kernel, shards),
            out_shape=jax.ShapeDtypeStruct((rows_dev, list_len), jnp.float32),
            in_specs=[pl.BlockSpec(memory_space=pltpu.SMEM), pl.BlockSpec(memory_space=pltpu.VMEM),
                      pl.BlockSpec(memory_space=pltpu.VMEM), pl.BlockSpec(memory_space=pltpu.VMEM)],
            out_specs=pl.BlockSpec(memory_space=pltpu.VMEM),
            scratch_shapes=[
                pltpu.VMEM((half, depth), w_head.dtype),
                pltpu.VMEM((n_wire * CHUNK, depth), w_head.dtype),
                pltpu.VMEM((pl.cdiv(n_all * CHUNK, SCORED) * SCORED, depth), w_head.dtype),
                pltpu.VMEM((pl.cdiv(n_all * CHUNK, SCORED) * SCORED, depth), w_head.dtype),
                pltpu.VMEM((2, 1, half), jnp.int32),
                pltpu.VMEM((CHUNK, 2 * CHUNK), jnp.bfloat16),
                pltpu.VMEM((CHUNK, depth), w_head.dtype),
                pltpu.VMEM((CHUNK, depth), w_head.dtype),
                pltpu.SemaphoreType.DMA((n_own,)),
                pltpu.SemaphoreType.DMA((n_own,)),
                pltpu.SemaphoreType.DMA((n_wire,)),
                pltpu.SemaphoreType.DMA((n_wire,)),
                pltpu.SemaphoreType.DMA((n_all,)),
                pltpu.SemaphoreType.DMA((n_all,)),
            ],
            compiler_params=pltpu.CompilerParams(collective_id=0, has_side_effects=True, vmem_limit_bytes=34 * 1024 * 1024),
            name='ring_scores',
        )(base, rank, hidden, gbuf)

        tile = 128
        probs, logp = pl.pallas_call(
            softmax_kernel,
            grid=(rows_dev // tile,),
            out_shape=[jax.ShapeDtypeStruct((rows_dev, list_len), jnp.float32), jax.ShapeDtypeStruct((rows_dev // tile, 1, tile), jnp.float32)],
            in_specs=[pl.BlockSpec(memory_space=pltpu.VMEM), pl.BlockSpec((1, list_len), lambda i: (0, 0)),
                      pl.BlockSpec((1, 1, tile), lambda i: (i, 0, 0))],
            out_specs=[pl.BlockSpec((tile, list_len), lambda i: (i, 0)), pl.BlockSpec((1, 1, tile), lambda i: (i, 0, 0))],
            compiler_params=pltpu.CompilerParams(vmem_limit_bytes=24 * 1024 * 1024),
            name='softmax',
        )(scores, allowed_valid.reshape(1, list_len), target_pos.reshape(rows_dev // tile, 1, tile))
        return probs, logp.reshape(rows_dev)

    row_spec = P(('rep', 'vocab'))
    mat_spec = P(('rep', 'vocab'), None)
    return jax.shard_map(device_step, mesh=mesh, in_specs=(mat_spec, P('vocab', None), P('rep'), P('rep'), row_spec), out_specs=(mat_spec, row_spec), check_vma=False)
```

profile of v0, /device:TPU:112, one launch (start us, length us, event | category | flops | bytes accessed | tf_op | source)
XLA Modules:
  0.0 98.1 jit_solution(10961117581336524897)
XLA Ops:
  0.6 0.7 lt.25
  1.3 0.3 fusion
  1.7 0.1 copy.7
  1.8 0.1 reduce_sum.30.base_ref
  1.9 1.0 convert_reduce_fusion.rank_ref
  2.8 1.0 %select_reduce_fusion.sid_ref = s32[2,1024]{1,0:T(2,128)S(1)} fusion(s32[2,1024]{1,0:T(2,128)S(1)} %convert_reduce_fusion.rank_ref, s32[2,1024]{1,0:T(2,128)S(1)} %lt.25), kind=kLoop, calls=%fused_computation | loop fusion | flops 6289408 | bytes 24576 | tf_op jit(solution)/shard_map/reduce_sum | solution.py:323
  3.9 0.0 copy-start
  3.9 0.8 gather_rows.1.gbuf_ref
  4.6 0.9 copy-done
  5.5 0.0 copy-start.1
  5.5 0.0 copy-start.2
  5.5 89.2 %ring_scores.1.s_ref = f32[512,2048]{1,0:T(8,128)S(1)} custom-call(s32[18]{0:T(128)S(1)} %reduce_sum.30.base_ref, s32[2,1024]{1,0:T(2,128)S(1)} %convert_reduce_fusion.rank_ref, bf16[512,2304]{1,0:T(8,128)(2,1)S(1)} %copy-done, bf16[2,1024,2304]{2,1,0:T(8,128)(2,1)S(1)} %gather_rows.1.gbuf_ref), custom_call_target="tpu_custom_call" | custom-call | tf_op jit(solution)/shard_map/ring_scores/pallas_call | solution.py:344
  94.7 0.0 copy-done.1
  94.7 0.0 copy-done.2
  94.7 3.3 %softmax.1 = (f32[512,2048]{1,0:T(8,128)}, f32[4,1,128]{2,1,0:T(1,128)}) custom-call(f32[512,2048]{1,0:T(8,128)S(1)} %ring_scores.1.s_ref, s32[1,2048]{1,0:T(1,128)S(1)} %bitcast.3, s32[4,1,128]{2,1,0:T(1,128)S(1)} %bitcast.4), custom_call_target="tpu_custom_call" | custom-call | tf_op jit(solution)/shard_map/softmax/pallas_call | solution.py:371
  (1 shorter events, 0.0 us)
Async XLA Ops:
  3.9 1.7 %copy-start = (bf16[512,2304]{1,0:T(8,128)(2,1)S(1)}, bf16[512,2304]{1,0:T(8,128)(2,1)}, u32[]{:S(2)}) copy-start(bf16[512,2304]{1,0:T(8,128)(2,1)} %hid.1) | copy-start | bytes 7077892
  5.5 89.2 %copy-start.1 = (s32[2048]{0:T(1024)S(1)}, s32[2048]{0:T(1024)}, u32[]{:S(2)}) copy-start(s32[2048]{0:T(1024)} %param.8) | copy-start | bytes 24580
  5.5 89.2 %copy-start.2 = (s32[512]{0:T(512)S(1)}, s32[512]{0:T(512)}, u32[]{:S(2)}) copy-start(s32[512]{0:T(512)} %param.9) | copy-start | bytes 6148
where the time goes:
time: 97.4 us; the launch traced here: 98.1 us
  Pallas kernels  93.2 us (96%)
  other arithmetic  2.34 us (2%)
  local copies, waits for them, and re-layouts  1.79 us (2%)
    pallas_call x1, Pallas kernels, device_step(): pl.pallas_call(functools.partial(ring_kernel, shards), out_shape=jax.Shap...  89.2 us
    pallas_call x1, Pallas kernels, device_step(): pl.pallas_call(softmax_kernel, grid=(rows_dev // tile,), out_shape=[jax.S...  3.34 us

commit v1 on v0

--- a/solution.py
+++ b/solution.py
@@ -20,10 +20,8 @@
 CUT = 768
 
 
-def gather_kernel(shards, base_ref, sid_ref, w_ref, gbuf_ref, stage, pick, in_sem):
+def gather_kernel(shards, base_ref, local_ref, w_ref, gbuf_ref, stage, pick, in_sem):
     v = lax.axis_index('vocab')
-    vocab_local = w_ref.shape[0]
-    half = gbuf_ref.shape[1]
     chip = v // 2
 
     def span(k):
@@ -33,20 +31,17 @@
         slot0 = first - base_ref[at + 2 * chip]
         block0 = slot0 // GATHER
         blocks = jnp.where(count > 0, (slot0 + count + GATHER - 1) // GATHER - block0, 0)
-        return first, count, slot0, block0, blocks
+        return first, slot0, block0, blocks
 
     spans = [span(0), span(1)]
-    total = spans[0][4] + spans[1][4]
+    total = spans[0][3] + spans[1][3]
 
     def where_is(t):
-        second = t >= spans[0][4]
-        first, count, slot0, block0 = [jnp.where(second, spans[1][i], spans[0][i]) for i in range(4)]
+        second = t >= spans[0][3]
+        first, slot0, block0 = [jnp.where(second, spans[1][i], spans[0][i]) for i in range(3)]
         k = jnp.where(second, 1, 0)
-        block = block0 + jnp.where(second, t - spans[0][4], t)
-        lo = jnp.maximum(slot0 - block * GATHER, 0)
-        last = jnp.minimum(slot0 + count - block * GATHER, GATHER) - 1
-        src = first + block * GATHER - slot0
-        return k, block, lo, last, src
+        block = block0 + jnp.where(second, t - spans[0][3], t)
+        return k, block, first - slot0 + block * GATHER
 
     def row_copy(group, s, b):
         return pltpu.make_async_copy(
@@ -57,9 +52,9 @@
     lane = lax.broadcasted_iota(jnp.int32, (1, GATHER * PACK), 1)
 
     def issue(t, b):
-        k, first, last, src = where_is(t)[0], *where_is(t)[2:]
+        k, _, src = where_is(t)
         for s in range(GATHER):
-            local = sid_ref[k, src + jnp.clip(s, first, last)] - v * vocab_local
+            local = local_ref[k, src + s]
             group = lax.shift_right_logical(local, PACK_BITS)
             row_copy(group, s, b).start()
             pick[b, pl.ds(s, 1), :] = jnp.where(lane == s * PACK + (local & (PACK - 1)), 1.0, 0.0)
@@ -79,7 +74,7 @@
             issue(t + STAGES - 1, lax.rem(t + STAGES - 1, STAGES))
 
         wait_stage(b)
-        k, block = where_is(t)[:2]
+        k, block, _ = where_is(t)
         gbuf_ref[k, pl.ds(pl.multiple_of(block * GATHER, GATHER), GATHER), :] = jnp.dot(
             pick[b].astype(jnp.bfloat16), stage[b].reshape(GATHER * PACK, stage.shape[3]),
             preferred_element_type=jnp.float32).astype(gbuf_ref.dtype)
@@ -102,6 +97,7 @@
     group = SCORED // CHUNK
     pad = -n_all % group
     gap = group // PIECES
+    final = n_all - 1 - group + gap
     depth = hid.shape[1]
     v = lax.axis_index('vocab')
     core = lax.rem(v, 2)
@@ -253,7 +249,7 @@
 
         since = e - (group - 1 - pad)
 
-        @pl.when((since >= gap) & (lax.rem(since, gap) == 0) & (e < n_all - 1))
+        @pl.when((since >= gap) & (lax.rem(since, gap) == 0) & (e <= final))
         def _():
             p = (since // gap - 1) // PIECES
             piece = lax.rem(since // gap - 1, PIECES)
@@ -266,7 +262,7 @@
                 score(p, pl.multiple_of(i * (n_rows // PIECES), n_rows // PIECES), n_rows // PIECES)
                 return c
 
-            lax.fori_loop(piece, jnp.where(e == n_all - 2, PIECES, piece + 1), one, 0)
+            lax.fori_loop(piece, jnp.where(e == final, PIECES, piece + 1), one, 0)
 
         return carry
 
@@ -319,8 +315,9 @@
         chips = shards // 2
         ids = allowed_ids.reshape(2, half)
         rank = jnp.sum((ids[:, :, None] < ids[:, None, :]).astype(jnp.int32), axis=1)
-        at = lax.broadcasted_iota(jnp.int32, (2, half, half), 1)
+        at = lax.broadcasted_iota(jnp.int32, (2, half + GATHER, half), 1)
         sorted_ids = jnp.sum(jnp.where(rank[:, None, :] == at, ids[:, None, :], 0), axis=2)
+        local = jnp.clip(sorted_ids - lax.axis_index('vocab') * vocab_local, 0, vocab_local - 1)
         edges = lax.broadcasted_iota(jnp.int32, (2, shards + 1, half), 1) * vocab_local
         base = jnp.sum((ids[:, None, :] < edges).astype(jnp.int32).reshape(2 * (shards + 1), half), axis=1)
 
@@ -336,7 +333,7 @@
             ],
             compiler_params=pltpu.CompilerParams(vmem_limit_bytes=20 * 1024 * 1024),
             name='gather_rows',
-        )(base, sorted_ids, w_head)
+        )(base, local, w_head)
 
         n_own = half // CHUNK
         n_wire = n_own + (chips - 2) * LAG
@@ -367,7 +364,7 @@
             name='ring_scores',
         )(base, rank, hidden, gbuf)
 
-        tile = 128
+        tile = 256
         probs, logp = pl.pallas_call(
             softmax_kernel,
             grid=(rows_dev // tile,),

time: 97.4 us -> 96.2 us (0.988)
  Pallas kernels: 93.2 us -> 92.1 us
    pallas_call x1, Pallas kernels: 89.2 us -> 83.6 us  [device_step(): pl.pallas_call(functools.partial(ring_kernel, shards), out_shape=jax.Shap...]
    pallas_call x1, Pallas kernels: 0.75 us -> 5.34 us  [device_step(): pl.pallas_call(functools.partial(gather_kernel, shards), out_shape=jax.Sh...]
where the time goes in v1:
time: 96.2 us; the launch traced here: 96.1 us
  Pallas kernels  92.1 us (96%)
  other arithmetic  2.4 us (2%)
    pallas_call x1, Pallas kernels, device_step(): pl.pallas_call(functools.partial(ring_kernel, shards), out_shape=jax.Shap...  83.6 us
    pallas_call x1, Pallas kernels, device_step(): pl.pallas_call(functools.partial(gather_kernel, shards), out_shape=jax.Sh...  5.34 us
    pallas_call x1, Pallas kernels, device_step(): pl.pallas_call(softmax_kernel, grid=(rows_dev // tile,), out_shape=[jax.S...  3.18 us

profile of v1, /device:TPU:112, one launch (start us, length us, event | category | flops | bytes accessed | tf_op | source)
XLA Modules:
  0.0 96.1 jit_solution(12477886610133233243)
XLA Ops:
  0.6 0.7 lt.25
  1.4 0.3 fusion
  1.7 0.1 copy.7
  1.8 0.1 reduce_sum.30.base_ref
  1.9 1.0 %convert_reduce_fusion.rank_ref = s32[2,1024]{1,0:T(2,128)S(1)} fusion(s32[2,1024]{1,0:T(2,128)S(1)} %lt.25), kind=kLoop, calls=%fused_computation.2 | loop fusion | flops 6289408 | bytes 16384 | tf_op jit(solution)/shard_map/reduce_sum | solution.py:317
  2.8 1.1 %select_reduce_fusion = s32[2,1056]{1,0:T(2,128)S(1)} fusion(s32[2,1024]{1,0:T(2,128)S(1)} %lt.25, s32[2,1024]{1,0:T(2,128)S(1)} %convert_reduce_fusion.rank_ref), kind=kLoop, calls=%fused_computation | loop fusion | flops 6485952 | bytes 24832 | tf_op jit(solution)/shard_map/reduce_sum | solution.py:319
  3.9 0.0 copy-start
  4.0 5.3 %gather_rows.1.gbuf_ref = bf16[2,1024,2304]{2,1,0:T(8,128)(2,1)S(1)} custom-call(s32[18]{0:T(128)S(1)} %reduce_sum.30.base_ref, s32[2,1056]{1,0:T(2,128)S(1)} %subtract_clamp_fusion.local_ref, bf16[32000,2304]{1,0:T(8,128)(2,1)} %w_ref.1), custom_call_target="tpu_custom_call" | custom-call | tf_op jit(solution)/shard_map/gather_rows/pallas_call | solution.py:324
  9.3 0.0 copy-done
  9.3 0.0 copy-start.1
  9.3 0.0 copy-start.2
  9.3 83.6 %ring_scores.1.s_ref = f32[512,2048]{1,0:T(8,128)S(1)} custom-call(s32[18]{0:T(128)S(1)} %reduce_sum.30.base_ref, s32[2,1024]{1,0:T(2,128)S(1)} %convert_reduce_fusion.rank_ref, bf16[512,2304]{1,0:T(8,128)(2,1)S(1)} %copy-done, bf16[2,1024,2304]{2,1,0:T(8,128)(2,1)S(1)} %gather_rows.1.gbuf_ref), custom_call_target="tpu_custom_call" | custom-call | tf_op jit(solution)/shard_map/ring_scores/pallas_call | solution.py:341
  92.9 0.0 copy-done.1
  92.9 0.0 copy-done.2
  92.9 3.2 %softmax.1 = (f32[512,2048]{1,0:T(8,128)}, f32[2,1,256]{2,1,0:T(1,128)}) custom-call(f32[512,2048]{1,0:T(8,128)S(1)} %ring_scores.1.s_ref, s32[1,2048]{1,0:T(1,128)S(1)} %bitcast.3, s32[2,1,256]{2,1,0:T(1,128)S(1)} %bitcast.4), custom_call_target="tpu_custom_call" | custom-call | tf_op jit(solution)/shard_map/softmax/pallas_call | solution.py:368
  (2 shorter events, 0.0 us)
Async XLA Ops:
  3.9 5.4 %copy-start = (bf16[512,2304]{1,0:T(8,128)(2,1)S(1)}, bf16[512,2304]{1,0:T(8,128)(2,1)}, u32[]{:S(2)}) copy-start(bf16[512,2304]{1,0:T(8,128)(2,1)} %hid.1) | copy-start | bytes 7077892
  9.3 83.6 %copy-start.1 = (s32[2048]{0:T(1024)S(1)}, s32[2048]{0:T(1024)}, u32[]{:S(2)}) copy-start(s32[2048]{0:T(1024)} %param.8) | copy-start | bytes 24580
  9.3 83.6 %copy-start.2 = (s32[512]{0:T(512)S(1)}, s32[512]{0:T(512)}, u32[]{:S(2)}) copy-start(s32[512]{0:T(512)} %param.9) | copy-start | bytes 6148

commit v2 on v1

--- a/solution.py
+++ b/solution.py
@@ -16,7 +16,7 @@
 PACK = 1 << PACK_BITS
 SCORED = 128
 PIECES = 2
-STAGES = 4
+STAGES = 6
 CUT = 768
 
 
@@ -269,9 +269,13 @@
     lax.fori_loop(0, n_all, step, 0)
 
     last = (n_all + pad) // group - 1
-    move(core, against(0, n_rows, merged[group_rows(last), :]), last, 0, n_rows)
     wait_theirs(last)
-    move(1 - core, against(0, n_rows, theirs[group_rows(last), :]), last, 0, n_rows)
+
+    def tail(i, c):
+        score(last, pl.multiple_of(i * (n_rows // PIECES), n_rows // PIECES), n_rows // PIECES)
+        return c
+
+    lax.fori_loop(0, PIECES, tail, 0)
 
     def finish(e, c):
         @pl.when(e < n_own)

time: 96.2 us -> 94.6 us (0.983)
  the two profiles are of different devices: /device:TPU:112 before, /device:TPU:121 now
where the time goes in v2:
time: 94.6 us; the launch traced here: 93.8 us
  Pallas kernels  89 us (94%)
  other arithmetic  2.4 us (3%)
  local copies, waits for them, and re-layouts  1.76 us (2%)
    pallas_call x1, Pallas kernels, device_step(): pl.pallas_call(functools.partial(ring_kernel, shards), out_shape=jax.Shap...  85 us
    pallas_call x1, Pallas kernels, device_step(): pl.pallas_call(softmax_kernel, grid=(rows_dev // tile,), out_shape=[jax.S...  3.18 us

profile of v2, /device:TPU:121, one launch (start us, length us, event | category | flops | bytes accessed | tf_op | source)
XLA Modules:
  0.0 93.8 jit_solution(3671721263626849846)
XLA Ops:
  0.6 0.7 lt.25
  1.4 0.3 fusion
  1.7 0.1 copy.7
  1.8 0.1 reduce_sum.30.base_ref
  1.9 1.0 %convert_reduce_fusion.rank_ref = s32[2,1024]{1,0:T(2,128)S(1)} fusion(s32[2,1024]{1,0:T(2,128)S(1)} %lt.25), kind=kLoop, calls=%fused_computation.2 | loop fusion | flops 6289408 | bytes 16384 | tf_op jit(solution)/shard_map/reduce_sum | solution.py:321
  2.8 1.1 %select_reduce_fusion = s32[2,1056]{1,0:T(2,128)S(1)} fusion(s32[2,1024]{1,0:T(2,128)S(1)} %lt.25, s32[2,1024]{1,0:T(2,128)S(1)} %convert_reduce_fusion.rank_ref), kind=kLoop, calls=%fused_computation | loop fusion | flops 6485952 | bytes 24832 | tf_op jit(solution)/shard_map/reduce_sum | solution.py:323
  3.9 0.0 copy-start
  4.0 0.8 gather_rows.1.gbuf_ref
  4.8 0.9 copy-done
  5.6 0.0 copy-start.1
  5.6 0.0 copy-start.2
  5.6 85.0 %ring_scores.1.s_ref = f32[512,2048]{1,0:T(8,128)S(1)} custom-call(s32[18]{0:T(128)S(1)} %reduce_sum.30.base_ref, s32[2,1024]{1,0:T(2,128)S(1)} %convert_reduce_fusion.rank_ref, bf16[512,2304]{1,0:T(8,128)(2,1)S(1)} %copy-done, bf16[2,1024,2304]{2,1,0:T(8,128)(2,1)S(1)} %gather_rows.1.gbuf_ref), custom_call_target="tpu_custom_call" | custom-call | tf_op jit(solution)/shard_map/ring_scores/pallas_call | solution.py:345
  90.6 0.0 copy-done.1
  90.6 0.0 copy-done.2
  90.7 3.2 %softmax.1 = (f32[512,2048]{1,0:T(8,128)}, f32[2,1,256]{2,1,0:T(1,128)}) custom-call(f32[512,2048]{1,0:T(8,128)S(1)} %ring_scores.1.s_ref, s32[1,2048]{1,0:T(1,128)S(1)} %bitcast.3, s32[2,1,256]{2,1,0:T(1,128)S(1)} %bitcast.4), custom_call_target="tpu_custom_call" | custom-call | tf_op jit(solution)/shard_map/softmax/pallas_call | solution.py:372
  (2 shorter events, 0.0 us)
Async XLA Ops:
  3.9 1.7 %copy-start = (bf16[512,2304]{1,0:T(8,128)(2,1)S(1)}, bf16[512,2304]{1,0:T(8,128)(2,1)}, u32[]{:S(2)}) copy-start(bf16[512,2304]{1,0:T(8,128)(2,1)} %hid.1) | copy-start | bytes 7077892
  5.6 85.0 %copy-start.1 = (s32[2048]{0:T(1024)S(1)}, s32[2048]{0:T(1024)}, u32[]{:S(2)}) copy-start(s32[2048]{0:T(1024)} %param.8) | copy-start | bytes 24580
  5.6 85.0 %copy-start.2 = (s32[512]{0:T(512)S(1)}, s32[512]{0:T(512)}, u32[]{:S(2)}) copy-start(s32[512]{0:T(512)} %param.9) | copy-start | bytes 6148

commit v3 on v2

--- a/solution.py
+++ b/solution.py
@@ -197,10 +197,6 @@
                 pair_copy(at).wait_recv()
 
     def step(e, carry):
-        @pl.when(e + ahead_of_use < n_own)
-        def _():
-            other_copy(e + ahead_of_use).start()
-
         @pl.when(e < n_own)
         def _():
             other_copy(e).wait_recv()
@@ -231,6 +227,10 @@
         @pl.when(e < n_wire)
         def _():
             ring_copy(e).start()
+
+        @pl.when(e + ahead_of_use < n_own)
+        def _():
+            other_copy(e + ahead_of_use).start()
 
         pair_copy(e).start()
 

time: 94.6 us -> 94.2 us (level)
  the two profiles are of different devices: /device:TPU:121 before, /device:TPU:112 now
where the time goes in v3:
time: 94.2 us; the launch traced here: 92.5 us
  Pallas kernels  88.4 us (94%)
  other arithmetic  2.4 us (3%)
    pallas_call x1, Pallas kernels, device_step(): pl.pallas_call(functools.partial(ring_kernel, shards), out_shape=jax.Shap...  79.1 us
    pallas_call x1, Pallas kernels, device_step(): pl.pallas_call(functools.partial(gather_kernel, shards), out_shape=jax.Sh...  6.18 us
    pallas_call x1, Pallas kernels, device_step(): pl.pallas_call(softmax_kernel, grid=(rows_dev // tile,), out_shape=[jax.S...  3.18 us

profile of v3, /device:TPU:112, one launch (start us, length us, event | category | flops | bytes accessed | tf_op | source)
XLA Modules:
  0.0 92.5 jit_solution(3557006264403170704)
XLA Ops:
  0.6 0.7 lt.25
  1.4 0.3 fusion
  1.7 0.1 copy.7
  1.8 0.1 reduce_sum.30.base_ref
  1.9 1.0 %convert_reduce_fusion.rank_ref = s32[2,1024]{1,0:T(2,128)S(1)} fusion(s32[2,1024]{1,0:T(2,128)S(1)} %lt.25), kind=kLoop, calls=%fused_computation.2 | loop fusion | flops 6289408 | bytes 16384 | tf_op jit(solution)/shard_map/reduce_sum | solution.py:321
  2.8 1.1 %select_reduce_fusion = s32[2,1056]{1,0:T(2,128)S(1)} fusion(s32[2,1024]{1,0:T(2,128)S(1)} %lt.25, s32[2,1024]{1,0:T(2,128)S(1)} %convert_reduce_fusion.rank_ref), kind=kLoop, calls=%fused_computation | loop fusion | flops 6485952 | bytes 24832 | tf_op jit(solution)/shard_map/reduce_sum | solution.py:323
  3.9 0.0 copy-start
  4.0 6.2 %gather_rows.1.gbuf_ref = bf16[2,1024,2304]{2,1,0:T(8,128)(2,1)S(1)} custom-call(s32[18]{0:T(128)S(1)} %reduce_sum.30.base_ref, s32[2,1056]{1,0:T(2,128)S(1)} %subtract_clamp_fusion.local_ref, bf16[32000,2304]{1,0:T(8,128)(2,1)} %w_ref.1), custom_call_target="tpu_custom_call" | custom-call | tf_op jit(solution)/shard_map/gather_rows/pallas_call | solution.py:328
  10.1 0.0 copy-done
  10.1 0.0 copy-start.1
  10.2 0.0 copy-start.2
  10.2 79.1 %ring_scores.1.s_ref = f32[512,2048]{1,0:T(8,128)S(1)} custom-call(s32[18]{0:T(128)S(1)} %reduce_sum.30.base_ref, s32[2,1024]{1,0:T(2,128)S(1)} %convert_reduce_fusion.rank_ref, bf16[512,2304]{1,0:T(8,128)(2,1)S(1)} %copy-done, bf16[2,1024,2304]{2,1,0:T(8,128)(2,1)S(1)} %gather_rows.1.gbuf_ref), custom_call_target="tpu_custom_call" | custom-call | tf_op jit(solution)/shard_map/ring_scores/pallas_call | solution.py:345
  89.3 0.0 copy-done.1
  89.3 0.0 copy-done.2
  89.3 3.2 %softmax.1 = (f32[512,2048]{1,0:T(8,128)}, f32[2,1,256]{2,1,0:T(1,128)}) custom-call(f32[512,2048]{1,0:T(8,128)S(1)} %ring_scores.1.s_ref, s32[1,2048]{1,0:T(1,128)S(1)} %bitcast.3, s32[2,1,256]{2,1,0:T(1,128)S(1)} %bitcast.4), custom_call_target="tpu_custom_call" | custom-call | tf_op jit(solution)/shard_map/softmax/pallas_call | solution.py:372
  (2 shorter events, 0.0 us)
Async XLA Ops:
  3.9 6.2 %copy-start = (bf16[512,2304]{1,0:T(8,128)(2,1)S(1)}, bf16[512,2304]{1,0:T(8,128)(2,1)}, u32[]{:S(2)}) copy-start(bf16[512,2304]{1,0:T(8,128)(2,1)} %hid.1) | copy-start | bytes 7077892
  10.1 79.1 %copy-start.1 = (s32[2048]{0:T(1024)S(1)}, s32[2048]{0:T(1024)}, u32[]{:S(2)}) copy-start(s32[2048]{0:T(1024)} %param.8) | copy-start | bytes 24580
  10.2 79.1 %copy-start.2 = (s32[512]{0:T(512)S(1)}, s32[512]{0:T(512)}, u32[]{:S(2)}) copy-start(s32[512]{0:T(512)} %param.9) | copy-start | bytes 6148
